TPU v7x, 32 devices: a whole 2x2x4 slice. The times are simulated.
32 devices in a mesh: bank: 4 (over z), zero: 8 (over y, x, core).
Axes of the slice: x: 2, y: 2, z: 4, core: 2. Of those that a mesh axis runs over, the one named last changes fastest.
Arguments:
- train_gate: float32 [64, 2048, 1408], P('bank', 'zero'), may hold values from -0.1875 to 0.1875
- train_up: float32 [64, 2048, 1408], P('bank', 'zero'), may hold values from -0.1875 to 0.1875
- router_weight: float32 [2048, 64], P('zero', 'bank'), may hold values from -0.125 to 0.125
- router_gain: float32 [2048], P('zero'), may hold values from 0.25 to 1.75
Outputs:
- ready_gate: bfloat16 [64, 2048, 1408], P('bank', None, 'zero')
- ready_up: bfloat16 [64, 2048, 1408], P('bank', None, 'zero')
- scale_gate: float32 [64, 1408], P('bank', 'zero')
- scale_up: float32 [64, 1408], P('bank', 'zero')
- serve_router: bfloat16 [2048, 64], replicated
All inputs are finite; a program needn't handle non-finite values. Where the computation divides by a largest or mean magnitude, that divisor is 1e-20 or more.
Results may differ from a plain program's by a relative error of at most 0.012.
Values may be sent and summed in bfloat16 or wider, within the bound.
A program may use at most 192 MiB of HBM per device.

v0:
```python
import jax
import jax.numpy as jnp
from jax import lax
from jax.sharding import PartitionSpec as P

D_MODEL = 2048


def local(train_gate, train_up, router_weight, router_gain):
    total_gate, total_up = (
        lax.psum(jnp.sum(jnp.abs(train_gate), axis=1).astype(jnp.bfloat16), "zero").astype(
            jnp.float32
        ),
        lax.psum(jnp.sum(jnp.abs(train_up), axis=1).astype(jnp.bfloat16), "zero").astype(
            jnp.float32
        ),
    )
    scale_gate = total_gate / D_MODEL
    scale_up = total_up / D_MODEL
    narrow_gate, narrow_up = (
        (train_gate / jnp.expand_dims(scale_gate, 1)).astype(jnp.bfloat16),
        (train_up / jnp.expand_dims(scale_up, 1)).astype(jnp.bfloat16),
    )
    ready_gate, ready_up = (
        lax.all_to_all(narrow_gate, "zero", split_axis=2, concat_axis=1, tiled=True),
        lax.all_to_all(narrow_up, "zero", split_axis=2, concat_axis=1, tiled=True),
    )
    scale_gate = lax.dynamic_slice_in_dim(
        scale_gate, lax.axis_index("zero") * ready_gate.shape[2], ready_gate.shape[2], axis=1
    )
    scale_up = lax.dynamic_slice_in_dim(
        scale_up, lax.axis_index("zero") * ready_up.shape[2], ready_up.shape[2], axis=1
    )
    part_router = (router_weight * router_gain[:, None]).astype(jnp.bfloat16)
    row_router = lax.all_gather(part_router, "zero", axis=0, tiled=True)
    serve_router = lax.all_gather(row_router, "bank", axis=1, tiled=True)
    return (ready_gate, ready_up, scale_gate, scale_up, serve_router)


def solution(mesh):
    in_specs = (P("bank", "zero", None), P("bank", "zero", None), P("zero", "bank"), P("zero"))
    out_specs = (
        P("bank", None, "zero"),
        P("bank", None, "zero"),
        P("bank", "zero"),
        P("bank", "zero"),
        P(),
    )
    return jax.shard_map(local, mesh=mesh, in_specs=in_specs, out_specs=out_specs, check_vma=False)
```

profile of v0, /device:TPU:1, one launch (start us, length us, event | category | flops | bytes accessed | tf_op | source)
XLA Modules:
  0.0 441.5 jit_solution(4854745292164101)
XLA Ops:
  7.2 0.0 all-reduce.3.cloned.1.call-start
  7.2 16.0 %abs_reduce_fusion = (bf16[16,1408]{1,0:T(8,128)(2,1)}, bf16[16,1408]{1,0:T(8,128)(2,1)}) fusion(f32[16,256,1408]{2,1,0:T(8,128)} %param.5, f32[16,256,1408]{2,1,0:T(8,128)} %param.4), kind=kLoop, calls=%fused_computation.1 | loop fusion | flops 23023616 | bytes 46227456 | tf_op jit(solution)/shard_map/reduce_sum | solution.py:14
  23.2 0.0 all-reduce.3.cloned.1.call-update
  23.2 23.7 %copy.22 = f32[16,256,1408]{1,0,2:T(8,128)} copy(f32[16,256,1408]{2,1,0:T(8,128)} %param.5) | data formatting | bytes 46137344 | tf_op args[1]
  46.9 30.7 %all-reduce.3.cloned.1.call-done = (bf16[16,1408]{1,0:T(8,128)(2,1)}, bf16[16,1408]{1,0:T(8,128)(2,1)}) async-done(((bf16[16,1408]{1,0:T(8,128)(2,1)}, bf16[16,1408]{1,0:T(8,128)(2,1)}), (bf16[16,1408]{1,0:T(8,128)(2,1)}, bf16[16,1408]{1,0:T(8,128)(2,1)})) %all-reduce.3.cloned.1.call-update) | async-done | bytes 90128 | tf_op jit(solution)/shard_map/psum | solution.py:11
  77.6 0.8 convert_multiply_fusion
  78.4 0.3 copy.21
  78.7 14.2 %divide_convert_fusion = bf16[16,256,1408]{1,0,2:T(8,128)(2,1)} fusion(f32[16,256,1408]{1,0,2:T(8,128)} %copy.22, f32[16,1408]{0,1:T(8,128)S(1)} %copy.21), kind=kLoop, calls=%fused_computation | loop fusion | flops 11534336 | bytes 34693120 | tf_op jit(solution)/shard_map/convert_element_type | solution.py:22
  92.9 5.3 %all-to-all-start.1 = ((bf16[16,256,1408]{1,0,2:T(8,128)(2,1)}), bf16[16,256,1408]{1,0,2:T(8,128)(2,1)}, u32[]{:S(2)}, u32[]{:S(2)}) async-start(bf16[16,256,1408]{1,0,2:T(8,128)(2,1)} %divide_convert_fusion), calls=%async_computation.1 | async-start | bytes 23068672 | tf_op jit(solution)/shard_map/all_to_all | solution.py:26
  98.2 23.7 %copy.18 = f32[16,256,1408]{1,0,2:T(8,128)} copy(f32[16,256,1408]{2,1,0:T(8,128)} %param.4) | data formatting | bytes 46137344 | tf_op args[0]
  121.9 0.3 copy.17
  122.1 0.0 copy-start.1
  122.2 14.2 %divide_convert_fusion.1 = bf16[16,256,1408]{1,0,2:T(8,128)(2,1)} fusion(f32[16,256,1408]{1,0,2:T(8,128)} %copy.18, f32[16,1408]{0,1:T(8,128)S(1)} %copy.17), kind=kLoop, calls=%fused_computation.2 | loop fusion | flops 11534336 | bytes 34693120 | tf_op jit(solution)/shard_map/convert_element_type | solution.py:21
  136.4 86.1 %all-to-all-done.1 = bf16[16,256,1408]{1,0,2:T(8,128)(2,1)} async-done(((bf16[16,256,1408]{1,0,2:T(8,128)(2,1)}), bf16[16,256,1408]{1,0,2:T(8,128)(2,1)}, u32[]{:S(2)}, u32[]{:S(2)}) %all-to-all-start.1) | async-done | bytes 11534368 | tf_op jit(solution)/shard_map/all_to_all | solution.py:26
  222.5 8.5 %all-to-all-start = ((bf16[16,256,1408]{1,0,2:T(8,128)(2,1)}), bf16[16,256,1408]{1,0,2:T(8,128)(2,1)}, u32[]{:S(2)}, u32[]{:S(2)}) async-start(bf16[16,256,1408]{1,0,2:T(8,128)(2,1)} %divide_convert_fusion.1), calls=%async_computation | async-start | bytes 23068672 | tf_op jit(solution)/shard_map/all_to_all | solution.py:25
  231.0 130.9 %all_gather.6 = bf16[2048,16]{0,1:T(8,128)(2,1)S(1)} all-gather(bf16[256,16]{0,1:T(8,128)(2,1)S(1)} %multiply_convert_fusion), channel_id=1, replica_groups=mesh['bank'=4,'zero'=8] {'zero'}, dimensions={0}, use_global_device_ids=true | all-gather | bytes 73728 | tf_op jit(solution)/shard_map/all_gather | solution.py:35
  361.9 12.1 %all_gather.7 = bf16[2048,64]{0,1:T(8,128)(2,1)S(1)} all-gather(bf16[2048,16]{0,1:T(8,128)(2,1)S(1)} %all_gather.6), channel_id=1, replica_groups=mesh['bank'=4,'zero'=8] {'bank'}, dimensions={1}, use_global_device_ids=true | all-gather | bytes 327680 | tf_op jit(solution)/shard_map/all_gather | solution.py:36
  374.0 0.7 constant_dynamic-slice_fusion
  374.7 0.7 constant_dynamic-slice_fusion.1
  375.4 11.4 %copy.24 = bf16[16,8,256,176]{2,1,3,0:T(8,128)(2,1)} copy(bf16[16,8,256,176]{2,0,3,1:T(8,128)(2,1)} %bitcast.5) | data formatting | bytes 23068672 | tf_op jit(solution)/shard_map/all_to_all | solution.py:26
  386.7 18.0 %all_to_all.33 = bf16[16,2048,176]{1,2,0:T(8,128)(2,1)} reshape(bf16[16,8,256,176]{2,1,3,0:T(8,128)(2,1)} %copy.24) | data formatting | bytes 23068672 | tf_op jit(solution)/shard_map/all_to_all | solution.py:26
  404.7 11.4 %copy.20 = bf16[16,8,256,176]{2,1,3,0:T(8,128)(2,1)} copy(bf16[16,8,256,176]{2,0,3,1:T(8,128)(2,1)} %bitcast.2) | data formatting | bytes 23068672 | tf_op jit(solution)/shard_map/all_to_all | solution.py:25
  416.0 18.0 %all_to_all.29 = bf16[16,2048,176]{1,2,0:T(8,128)(2,1)} reshape(bf16[16,8,256,176]{2,1,3,0:T(8,128)(2,1)} %copy.20) | data formatting | bytes 23068672 | tf_op jit(solution)/shard_map/all_to_all | solution.py:25
  434.0 0.7 copy.30
  (8 shorter events, 0.0 us)
Async XLA Ops:
  7.2 70.4 %all-reduce.3.cloned.1.call-start = ((), (), s32[]{:S(2)}) async-start(), calls=%async_computation.2 | async-start | bytes 180224 | tf_op jit(solution)/shard_map/psum | solution.py:11
  92.9 129.6 %all-to-all-start.1 = ((bf16[16,256,1408]{1,0,2:T(8,128)(2,1)}), bf16[16,256,1408]{1,0,2:T(8,128)(2,1)}, u32[]{:S(2)}, u32[]{:S(2)}) async-start(bf16[16,256,1408]{1,0,2:T(8,128)(2,1)} %divide_convert_fusion), calls=%async_computation.1 | async-start | bytes 23068672 | tf_op jit(solution)/shard_map/all_to_all | solution.py:26
  98.2 23.7 %copy-start = (bf16[16,1408]{1,0:T(8,128)(2,1)S(1)}, bf16[16,1408]{1,0:T(8,128)(2,1)}, u32[]{:S(2)}) copy-start(bf16[16,1408]{1,0:T(8,128)(2,1)} %get-tuple-element.5) | copy-start | bytes 135172
  122.1 108.9 %copy-start.1 = (f32[256,16]{0,1:T(8,128)S(1)}, f32[256,16]{0,1:T(8,128)}, u32[]{:S(2)}) copy-start(f32[256,16]{0,1:T(8,128)} %param.6) | copy-start | bytes 49156
  122.2 108.9 %copy-start.2 = (f32[256]{0:T(256)S(1)}, f32[256]{0:T(256)}, u32[]{:S(2)}) copy-start(f32[256]{0:T(256)} %param.7) | copy-start | bytes 3076
  222.5 182.2 %all-to-all-start = ((bf16[16,256,1408]{1,0,2:T(8,128)(2,1)}), bf16[16,256,1408]{1,0,2:T(8,128)(2,1)}, u32[]{:S(2)}, u32[]{:S(2)}) async-start(bf16[16,256,1408]{1,0,2:T(8,128)(2,1)} %divide_convert_fusion.1), calls=%async_computation | async-start | bytes 23068672 | tf_op jit(solution)/shard_map/all_to_all | solution.py:25
Sparse Core Ops, SparseCore 0:
  23.4 54.1 all-reduce.2
where the time goes:
time: 446 us; the launch traced here: 442 us
  blocking collectives  143 us (32%)
  waiting for transfers between devices  117 us (26%)
  local copies, waits for them, and re-layouts  109 us (24%)
  other arithmetic  45.3 us (10%)
  between operations  14.1 us (3%)
  starting transfers between devices  13.9 us (3%)
    all_gather x1, blocking collectives, local(): row_router = lax.all_gather(part_router, 'zero', axis=0, tiled=True)  131 us
    all_to_all x1, waiting for transfers between devices, local(): lax.all_to_all(narrow_up, 'zero', split_axis=2, concat_axis=1, tiled=True)  86.1 us
    unnamed x9, local copies, waits for them, and re-layouts  48.1 us
    psum x1, waiting for transfers between devices, local(): lax.psum(jnp.sum(jnp.abs(train_gate), axis=1).astype(jnp.bfloat16), 'zero')  30.7 us
    all_to_all x2, local copies, waits for them, and re-layouts, local(): lax.all_to_all(narrow_gate, 'zero', split_axis=2, concat_axis=1, tiled=True)  29.3 us
    all_to_all x2, local copies, waits for them, and re-layouts, local(): lax.all_to_all(narrow_up, 'zero', split_axis=2, concat_axis=1, tiled=True)  29.3 us
    reduce_sum x1, other arithmetic, local(): jnp.sum(jnp.abs(train_up), axis=1).astype(jnp.bfloat16)  16 us
    convert_element_type x1, other arithmetic, local(): (train_up / jnp.expand_dims(scale_up, 1)).astype(jnp.bfloat16)  14.2 us
  transfers between devices with their start and end apart: 3, of which 2 were waited for; matrix products, arithmetic and copies ran while one was open for 17% of the time, Pallas kernels for 0%

commit v1 on v0

v1 whole, which is shorter than its diff:
```python
import functools

import jax
import jax.numpy as jnp
from jax import lax
from jax.experimental import pallas as pl
from jax.experimental.pallas import tpu as pltpu
from jax.sharding import PartitionSpec as P

MESH = pl.DeviceIdType.MESH
LANES = 128
SLOTS = 8


def exchange(
    n, nb, gate, up, weight, gain, recv, router, inbuf, turned, send, part,
    in_sem, own_sem, send_sem, recv_sem, bank_send, bank_recv, zero_send, zero_recv,
):
    experts, rows, cols = gate.shape
    width = cols // n
    steps = 2 * experts
    slots = send.shape[0]
    me = lax.axis_index("zero")
    bank = lax.axis_index("bank")

    def fetch(source, e, slot):
        return pltpu.make_async_copy(source.at[e], inbuf.at[slot], in_sem.at[slot])

    fetch(gate, 0, 0).start()
    fetch(up, 0, 1).start()

    barrier = pltpu.get_barrier_semaphore()
    for k in range(1, n):
        pl.semaphore_signal(barrier, inc=1, device_id={"zero": lax.rem(me + k, n)}, device_id_type=MESH)
    for k in range(1, nb):
        pl.semaphore_signal(barrier, inc=1, device_id={"bank": lax.rem(bank + k, nb)}, device_id_type=MESH)
    part[...] = (weight[...] * gain[...]).astype(part.dtype)

    def own_copy(t, slot):
        return pltpu.make_async_copy(send.at[slot, me], recv.at[me, t], own_sem.at[slot])

    def peer_copy(t, slot, k):
        peer = lax.rem(me + k, n)
        return pltpu.make_async_remote_copy(
            src_ref=send.at[slot, peer],
            dst_ref=recv.at[me, t],
            send_sem=send_sem.at[slot, k],
            recv_sem=recv_sem.at[k],
            device_id={"zero": peer},
            device_id_type=MESH,
        )

    def turn(half, slot):
        for j in range(0, cols, LANES):
            turned[j : j + LANES, :] = inbuf[half, :, j : j + LANES].T
        for d in range(n):
            send[slot, d] = turned[d * width : (d + 1) * width, :].astype(send.dtype)

    def drain(t, slot):
        own_copy(t, slot).wait()
        for k in range(1, n):
            peer_copy(t, slot, k).wait_send()

    def launch(t, slot):
        for k in range(1, n):
            peer_copy(t, slot, k).start()
        own_copy(t, slot).start()

    def column(z):
        return pl.ds(pl.multiple_of(z * rows, rows), rows)

    def bank_copy(k):
        return pltpu.make_async_remote_copy(
            src_ref=part,
            dst_ref=router.at[bank, :, column(me)],
            send_sem=bank_send.at[k],
            recv_sem=bank_recv.at[k],
            device_id={"bank": lax.rem(bank + k, nb)},
            device_id_type=MESH,
        )

    def zero_copy(k):
        return pltpu.make_async_remote_copy(
            src_ref=router.at[:, :, column(me)],
            dst_ref=router.at[:, :, column(me)],
            send_sem=zero_send.at[k],
            recv_sem=zero_recv.at[k],
            device_id={"zero": lax.rem(me + k, n)},
            device_id_type=MESH,
        )

    fetch(gate, 0, 0).wait()
    turn(0, 0)
    pl.semaphore_wait(barrier, n - 1 + nb - 1)

    router[bank, :, column(me)] = part[...]
    for k in range(1, nb):
        bank_copy(k).start()

    @pl.loop(0, experts)
    def _(e):
        for half, source in enumerate((gate, up)):
            t = 2 * e + half
            slot = lax.rem(t, slots)

            def ready():
                fetch(source, e, half).wait()

                @pl.when(t >= slots)
                def _():
                    drain(t - slots, slot)

                turn(half, slot)

            if half == 0:
                pl.when(e > 0)(ready)
            else:
                ready()
            launch(t, slot)

            @pl.when(e + 1 < experts)
            def _():
                fetch(source, e + 1, half).start()

        @pl.when(e == min(1, experts - 1))
        def _():
            for k in range(1, nb):
                bank_copy(k).wait()
            for k in range(1, n):
                zero_copy(k).start()

    for k in range(1, n):
        zero_copy(k).wait()

    @pl.loop(max(steps - slots, 0), steps)
    def _(t):
        drain(t, lax.rem(t, slots))

    for k in range(1, n):
        source = lax.rem(me - k + n, n)
        pltpu.make_async_remote_copy(
            src_ref=recv.at[source],
            dst_ref=recv.at[source],
            send_sem=send_sem.at[0, 0],
            recv_sem=recv_sem.at[k],
            device_id={"zero": source},
            device_id_type=MESH,
        ).wait_recv()


def finish(n, d_model, got, ready_gate, ready_up, scale_gate, scale_up, wide):
    e = pl.program_id(0)
    width, rows = got.shape[2], got.shape[3]
    for half, (ready, scale) in enumerate(((ready_gate, scale_gate), (ready_up, scale_up))):
        total = jnp.zeros((width, LANES), jnp.float32)
        for s in range(n):
            for j in range(0, rows, LANES):
                total += jnp.abs(got[s, half, :, j : j + LANES].astype(jnp.float32))
        mean = jnp.sum(total, axis=1, keepdims=True) / d_model
        wide[0:width, :] = jnp.broadcast_to(mean, (width, LANES))
        for j in range(0, width, LANES):
            stop = min(j + LANES, width)
            line = wide[j : j + LANES, :].T[0:1, 0 : stop - j]
            mine = lax.broadcasted_iota(jnp.int32, (scale.shape[0], stop - j), 0) == e
            scale[:, j:stop] = jnp.where(mine, line, scale[:, j:stop])
        inverse = jnp.broadcast_to(1.0 / mean, (width, LANES))
        for s in range(n):
            for j in range(0, rows, LANES):
                value = got[s, half, :, j : j + LANES].astype(jnp.float32) * inverse
                ready[0, :, s * rows + j : s * rows + j + LANES] = value.astype(ready.dtype)


def solution(mesh):
    n, nb = mesh.shape["zero"], mesh.shape["bank"]

    def local(train_gate, train_up, router_weight, router_gain):
        experts, rows, cols = train_gate.shape
        width = cols // n
        d_model = rows * n
        mine = router_weight.shape[1]
        slots = min(SLOTS, 2 * experts)
        anywhere = pl.BlockSpec(memory_space=pl.ANY)
        inside = pl.BlockSpec(memory_space=pltpu.VMEM)
        recv, router = pl.pallas_call(
            functools.partial(exchange, n, nb),
            out_shape=(
                jax.ShapeDtypeStruct((n, 2 * experts, width, rows), jnp.bfloat16),
                jax.ShapeDtypeStruct((nb, mine, d_model), jnp.bfloat16),
            ),
            in_specs=[anywhere, anywhere, inside, inside],
            out_specs=(anywhere, inside),
            scratch_shapes=[
                pltpu.VMEM((2, rows, cols), jnp.float32),
                pltpu.VMEM((cols, rows), jnp.float32),
                pltpu.VMEM((slots, n, width, rows), jnp.bfloat16),
                pltpu.VMEM((mine, rows), jnp.bfloat16),
                pltpu.SemaphoreType.DMA((2,)),
                pltpu.SemaphoreType.DMA((slots,)),
                pltpu.SemaphoreType.DMA((slots, n)),
                pltpu.SemaphoreType.DMA((n,)),
                pltpu.SemaphoreType.DMA((nb,)),
                pltpu.SemaphoreType.DMA((nb,)),
                pltpu.SemaphoreType.DMA((n,)),
                pltpu.SemaphoreType.DMA((n,)),
            ],
            compiler_params=pltpu.CompilerParams(collective_id=0, has_side_effects=True),
        )(train_gate, train_up, router_weight.T, router_gain[None, :])

        padded = -(-width // LANES) * LANES
        ready = jax.ShapeDtypeStruct((experts, width, d_model), jnp.bfloat16)
        scale = jax.ShapeDtypeStruct((experts, width), jnp.float32)
        ready_spec = pl.BlockSpec((1, width, d_model), lambda e: (e, 0, 0))
        scale_spec = pl.BlockSpec((experts, width), lambda e: (0, 0))
        ready_gate, ready_up, scale_gate, scale_up = pl.pallas_call(
            functools.partial(finish, n, d_model),
            grid=(experts,),
            out_shape=(ready, ready, scale, scale),
            in_specs=[pl.BlockSpec((n, 2, width, rows), lambda e: (0, e, 0, 0))],
            out_specs=(ready_spec, ready_spec, scale_spec, scale_spec),
            scratch_shapes=[pltpu.VMEM((padded, LANES), jnp.float32)],
        )(recv)
        return (
            jnp.swapaxes(ready_gate, 1, 2),
            jnp.swapaxes(ready_up, 1, 2),
            scale_gate,
            scale_up,
            router.reshape(nb * mine, d_model).T,
        )

    in_specs = (P("bank", "zero", None), P("bank", "zero", None), P("zero", "bank"), P("zero"))
    out_specs = (
        P("bank", None, "zero"),
        P("bank", None, "zero"),
        P("bank", "zero"),
        P("bank", "zero"),
        P(),
    )
    return jax.shard_map(local, mesh=mesh, in_specs=in_specs, out_specs=out_specs, check_vma=False)
```

time: 446 us -> 286 us (0.64)
  Pallas kernels: 0 us -> 284 us
  blocking collectives: 143 us -> 0 us
  waiting for transfers between devices: 117 us -> 0 us
  local copies, waits for them, and re-layouts: 109 us -> 0.71 us
  other arithmetic: 45.3 us -> 0 us
  starting transfers between devices: 13.9 us -> 0 us
  between operations: 14.1 us -> 0.65 us
    pallas_call x0 -> x2, Pallas kernels: none -> 284 us  [the longest x1 260 us: local(): pl.pallas_call(functools.partial(exchange, n, nb), out_shape=(jax.ShapeDt...]
    all_gather x2 -> x0, blocking collectives: 143 us -> none  [the longest x1 131 us: local(): row_router = lax.all_gather(part_router, 'zero', axis=0, tiled=True)]
    all_to_all x2 -> x0, waiting for transfers between devices: 86.1 us -> none  [the longest x1 86.1 us: local(): lax.all_to_all(narrow_up, 'zero', split_axis=2, concat_axis=1, tiled=True)]
    all_to_all x4 -> x0, local copies, waits for them, and re-layouts: 58.6 us -> none  [the longest x2 29.3 us: local(): lax.all_to_all(narrow_gate, 'zero', split_axis=2, concat_axis=1, tiled=True)]
    unnamed x9 -> x3, local copies, waits for them, and re-layouts: 48.1 us -> 0.71 us
    psum x1 -> x0, waiting for transfers between devices: 30.7 us -> none  [local(): lax.psum(jnp.sum(jnp.abs(train_gate), axis=1).astype(jnp.bfloat16), 'zero')]
    convert_element_type x3 -> x0, other arithmetic: 28.4 us -> none  [the longest x1 14.2 us: local(): (train_up / jnp.expand_dims(scale_up, 1)).astype(jnp.bfloat16)]
    reduce_sum x1 -> x0, other arithmetic: 16 us -> none  [local(): jnp.sum(jnp.abs(train_up), axis=1).astype(jnp.bfloat16)]
  transfers between devices with their start and end apart: 3 -> 0, of which waited for: 2 -> 0; matrix products, arithmetic and copies ran while one was open for 17% -> 0% of each run, Pallas kernels for 0% -> 0%
where the time goes in v1:
time: 286 us; the launch traced here: 285 us
  Pallas kernels  284 us (99%)
    pallas_call x1, Pallas kernels, local(): pl.pallas_call(functools.partial(exchange, n, nb), out_shape=(jax.ShapeDt...  260 us
    pallas_call x1, Pallas kernels, local(): pl.pallas_call(functools.partial(finish, n, d_model), grid=(experts,), ou...  23.7 us

profile of v1, /device:TPU:1, one launch (start us, length us, event | category | flops | bytes accessed | tf_op | source)
XLA Modules:
  0.0 285.2 jit_solution(2479717165123737402)
XLA Ops:
  0.6 260.1 %shard_map.83 = (bf16[8,32,176,256]{3,2,1,0:T(8,128)(2,1)}, bf16[4,16,2048]{2,1,0:T(8,128)(2,1)}) custom-call(f32[16,256,1408]{2,1,0:T(8,128)} %gate.1, f32[16,256,1408]{2,1,0:T(8,128)} %up.1, f32[16,256]{1,0:T(8,128)} %bitcast.8, f32[1,256]{1,0:T(1,128)} %bitcast.9), custom_call_target="tpu_custom_call" | custom-call | tf_op jit(solution)/shard_map/pallas_call | solution.py:184
  260.8 0.0 copy-start
  260.8 23.7 %shard_map.84 = (bf16[16,176,2048]{2,1,0:T(8,128)(2,1)}, bf16[16,176,2048]{2,1,0:T(8,128)(2,1)}, f32[16,176]{1,0:T(8,128)}, f32[16,176]{1,0:T(8,128)}) custom-call(bf16[8,32,176,256]{3,2,1,0:T(8,128)(2,1)} %get-tuple-element.11.got), custom_call_target="tpu_custom_call" | custom-call | tf_op jit(solution)/shard_map/pallas_call | solution.py:214
  284.5 0.0 copy-done
  284.5 0.7 copy.10
Async XLA Ops:
  260.8 23.7 %copy-start = (bf16[4,16,2048]{2,1,0:T(8,128)(2,1)S(1)}, bf16[4,16,2048]{2,1,0:T(8,128)(2,1)}, u32[]{:S(2)}) copy-start(bf16[4,16,2048]{2,1,0:T(8,128)(2,1)} %get-tuple-element.16) | copy-start | bytes 786436

commit v2 on v1

v2 whole, which is shorter than its diff:
```python
import functools

import jax
import jax.numpy as jnp
from jax import lax
from jax.experimental import pallas as pl
from jax.experimental.pallas import tpu as pltpu
from jax.sharding import PartitionSpec as P

MESH = pl.DeviceIdType.MESH
LANES = 128
SLOTS = 8
LAG = 5
KERNEL_VMEM = 28 * 2**20
FINISH_VMEM = 2 * 2**20


def exchange(
    n, nb, gate, up, weight, gain, recv, router, scale_gate, scale_up, inbuf, turned, send, part, wide,
    in_sem, send_sem, recv_sem, bank_send, bank_recv, zero_send, zero_recv,
):
    experts, rows, cols = gate.shape
    width = cols // n
    steps = 2 * experts
    slots = send.shape[0]
    lag = min(LAG, experts)
    me = lax.axis_index("zero")
    bank = lax.axis_index("bank")

    def fetch(source, e, slot):
        return pltpu.make_async_copy(source.at[e], inbuf.at[slot], in_sem.at[slot])

    fetch(gate, 0, 0).start()
    fetch(up, 0, 1).start()

    barrier = pltpu.get_barrier_semaphore()
    for k in range(1, n):
        pl.semaphore_signal(barrier, inc=1, device_id={"zero": lax.rem(me + k, n)}, device_id_type=MESH)
    for k in range(1, nb):
        pl.semaphore_signal(barrier, inc=1, device_id={"bank": lax.rem(bank + k, nb)}, device_id_type=MESH)
    scale_gate[...] = jnp.zeros_like(scale_gate)
    scale_up[...] = jnp.zeros_like(scale_up)
    part[...] = (weight[...] * gain[...]).astype(part.dtype)

    def peer_copy(half, e, slot, k):
        peer = lax.rem(me + k, n)
        return pltpu.make_async_remote_copy(
            src_ref=send.at[slot, peer],
            dst_ref=recv.at[me, half, e],
            send_sem=send_sem.at[slot, k],
            recv_sem=recv_sem.at[e, k],
            device_id={"zero": peer},
            device_id_type=MESH,
        )

    def turn(half, slot):
        for j in range(0, cols, LANES):
            turned[j : j + LANES, :] = inbuf[half, :, j : j + LANES].T
        for d in range(n):
            send[slot, d] = turned[d * width : (d + 1) * width, :].astype(send.dtype)

    def drain(slot):
        for k in range(1, n):
            peer_copy(0, 0, slot, k).wait_send()

    def launch(half, e, slot):
        for k in range(1, n):
            peer_copy(half, e, slot, k).start()
        recv[me, half, e] = send[slot, me]

    def settle(e):
        for k in range(1, n):
            source = lax.rem(me - k + n, n)
            pltpu.make_async_remote_copy(
                src_ref=recv.at[source, :, e],
                dst_ref=recv.at[source, :, e],
                send_sem=send_sem.at[0, 0],
                recv_sem=recv_sem.at[e, k],
                device_id={"zero": source},
                device_id_type=MESH,
            ).wait_recv()
        for half, scale in enumerate((scale_gate, scale_up)):
            total = jnp.zeros((width, LANES), jnp.float32)
            for s in range(n):
                for j in range(0, rows, LANES):
                    total += jnp.abs(recv[s, half, e, :, j : j + LANES].astype(jnp.float32))
            mean = jnp.sum(total, axis=1, keepdims=True) / (rows * n)
            wide[0:width, :] = jnp.broadcast_to(mean, (width, LANES))
            for j in range(0, width, LANES):
                stop = min(j + LANES, width)
                line = wide[j : j + LANES, :].T[0:1, 0 : stop - j]
                here = lax.broadcasted_iota(jnp.int32, (experts, stop - j), 0) == e
                scale[:, j:stop] = jnp.where(here, line, scale[:, j:stop])
            inverse = jnp.broadcast_to(1.0 / mean, (width, LANES))
            for s in range(n):
                for j in range(0, rows, LANES):
                    value = recv[s, half, e, :, j : j + LANES].astype(jnp.float32) * inverse
                    recv[s, half, e, :, j : j + LANES] = value.astype(recv.dtype)

    def column(z):
        return pl.ds(pl.multiple_of(z * rows, rows), rows)

    def bank_copy(k):
        return pltpu.make_async_remote_copy(
            src_ref=part,
            dst_ref=router.at[bank, :, column(me)],
            send_sem=bank_send.at[k],
            recv_sem=bank_recv.at[k],
            device_id={"bank": lax.rem(bank + k, nb)},
            device_id_type=MESH,
        )

    def zero_copy(k):
        return pltpu.make_async_remote_copy(
            src_ref=router.at[:, :, column(me)],
            dst_ref=router.at[:, :, column(me)],
            send_sem=zero_send.at[k],
            recv_sem=zero_recv.at[k],
            device_id={"zero": lax.rem(me + k, n)},
            device_id_type=MESH,
        )

    fetch(gate, 0, 0).wait()
    turn(0, 0)
    pl.semaphore_wait(barrier, n - 1 + nb - 1)

    router[bank, :, column(me)] = part[...]
    for k in range(1, nb):
        bank_copy(k).start()

    @pl.loop(0, experts)
    def _(e):
        for half, source in enumerate((gate, up)):
            t = 2 * e + half
            slot = lax.rem(t, slots)

            def ready():
                fetch(source, e, half).wait()

                @pl.when(t >= slots)
                def _():
                    drain(slot)

                turn(half, slot)

            if half == 0:
                pl.when(e > 0)(ready)
            else:
                ready()
            launch(half, e, slot)

            @pl.when(e + 1 < experts)
            def _():
                fetch(source, e + 1, half).start()

        @pl.when(e == min(1, experts - 1))
        def _():
            for k in range(1, nb):
                bank_copy(k).wait()
            for k in range(1, n):
                zero_copy(k).start()

        @pl.when(e >= lag)
        def _():
            settle(e - lag)

    @pl.loop(experts - lag, experts)
    def _(e):
        settle(e)

    for k in range(1, n):
        zero_copy(k).wait()

    @pl.loop(max(steps - slots, 0), steps)
    def _(t):
        drain(lax.rem(t, slots))


def finish(
    recv, router, scale_gate, scale_up,
    ready_gate, ready_up, router_out, scale_gate_out, scale_up_out, sem, router_sem,
):
    n, rows = recv.shape[0], recv.shape[4]
    copies = [
        pltpu.make_async_copy(recv.at[s, half], ready.at[:, :, s * rows : (s + 1) * rows], sem.at[s, half])
        for s in range(n)
        for half, ready in enumerate((ready_gate, ready_up))
    ]
    copies.append(pltpu.make_async_copy(router, router_out, router_sem))
    for copy in copies:
        copy.start()
    scale_gate_out[...] = scale_gate[...]
    scale_up_out[...] = scale_up[...]
    for copy in copies:
        copy.wait()


def solution(mesh):
    n, nb = mesh.shape["zero"], mesh.shape["bank"]

    def local(train_gate, train_up, router_weight, router_gain):
        experts, rows, cols = train_gate.shape
        width = cols // n
        d_model = rows * n
        mine = router_weight.shape[1]
        slots = min(SLOTS, 2 * experts)
        anywhere = pl.BlockSpec(memory_space=pl.ANY)
        inside = pl.BlockSpec(memory_space=pltpu.VMEM)
        padded = -(-width // LANES) * LANES
        scale = jax.ShapeDtypeStruct((experts, width), jnp.float32)
        joined = jax.ShapeDtypeStruct((nb, mine, d_model), jnp.bfloat16)
        recv, router, scale_gate, scale_up = pl.pallas_call(
            functools.partial(exchange, n, nb),
            out_shape=(
                jax.ShapeDtypeStruct((n, 2, experts, width, rows), jnp.bfloat16),
                joined,
                scale,
                scale,
            ),
            in_specs=[anywhere, anywhere, inside, inside],
            out_specs=(inside,) * 4,
            scratch_shapes=[
                pltpu.VMEM((2, rows, cols), jnp.float32),
                pltpu.VMEM((cols, rows), jnp.float32),
                pltpu.VMEM((slots, n, width, rows), jnp.bfloat16),
                pltpu.VMEM((mine, rows), jnp.bfloat16),
                pltpu.VMEM((padded, LANES), jnp.float32),
                pltpu.SemaphoreType.DMA((2,)),
                pltpu.SemaphoreType.DMA((slots, n)),
                pltpu.SemaphoreType.DMA((experts, n)),
                pltpu.SemaphoreType.DMA((nb,)),
                pltpu.SemaphoreType.DMA((nb,)),
                pltpu.SemaphoreType.DMA((n,)),
                pltpu.SemaphoreType.DMA((n,)),
            ],
            compiler_params=pltpu.CompilerParams(
                collective_id=0, has_side_effects=True, vmem_limit_bytes=KERNEL_VMEM
            ),
        )(train_gate, train_up, router_weight.T, router_gain[None, :])

        ready = jax.ShapeDtypeStruct((experts, width, d_model), jnp.bfloat16)
        ready_gate, ready_up, router, scale_gate, scale_up = pl.pallas_call(
            finish,
            out_shape=(ready, ready, joined, scale, scale),
            in_specs=[inside] * 4,
            out_specs=(anywhere, anywhere, anywhere, inside, inside),
            scratch_shapes=[pltpu.SemaphoreType.DMA((n, 2)), pltpu.SemaphoreType.DMA],
            compiler_params=pltpu.CompilerParams(vmem_limit_bytes=FINISH_VMEM),
        )(recv, router, scale_gate, scale_up)
        return (
            jnp.swapaxes(ready_gate, 1, 2),
            jnp.swapaxes(ready_up, 1, 2),
            scale_gate,
            scale_up,
            router.reshape(nb * mine, d_model).T,
        )

    in_specs = (P("bank", "zero", None), P("bank", "zero", None), P("zero", "bank"), P("zero"))
    out_specs = (
        P("bank", None, "zero"),
        P("bank", None, "zero"),
        P("bank", "zero"),
        P("bank", "zero"),
        P(),
    )
    return jax.shard_map(local, mesh=mesh, in_specs=in_specs, out_specs=out_specs, check_vma=False)
```

time: 286 us -> 271 us (0.948)
  Pallas kernels: 284 us -> 269 us
    pallas_call x1, Pallas kernels: 23.7 us -> 8.52 us  [local(): pl.pallas_call(finish, out_shape=(ready, ready, joined, scale, scale), in...]
where the time goes in v2:
time: 271 us
  Pallas kernels  269 us (99%)
    pallas_call x1, Pallas kernels, local(): pl.pallas_call(functools.partial(exchange, n, nb), out_shape=(jax.ShapeDt...  260 us
    pallas_call x1, Pallas kernels, local(): pl.pallas_call(finish, out_shape=(ready, ready, joined, scale, scale), in...  8.52 us

profile of v2, /device:TPU:1, one launch (start us, length us, event | category | flops | bytes accessed | tf_op | source)
XLA Modules:
  0.0 271.0 jit_solution(7875785527792231013)
XLA Ops:
  0.6 0.0 copy-start
  0.6 0.7 copy-done
  1.4 0.0 copy-start.1
  1.4 0.7 copy-done.1
  2.0 260.4 %shard_map.83 = (bf16[8,2,16,176,256]{4,3,2,1,0:T(8,128)(2,1)S(1)}, bf16[4,16,2048]{2,1,0:T(8,128)(2,1)S(1)}, f32[16,176]{1,0:T(8,128)S(1)}, f32[16,176]{1,0:T(8,128)S(1)}) custom-call(f32[16,256,1408]{2,1,0:T(8,128)} %gate.1, f32[16,256,1408]{2,1,0:T(8,128)} %up.1, f32[16,256]{1,0:T(8,128)S(1)} %bitcast.7, f32[1,256]{1,0:T(1,128)S(1)} %bitcast.8), custom_call_target="tpu_custom_call" | custom-call | tf_op jit(solution)/shard_map/pallas_call | solution.py:212
  262.4 8.5 %shard_map.84 = (bf16[16,176,2048]{2,1,0:T(8,128)(2,1)}, bf16[16,176,2048]{2,1,0:T(8,128)(2,1)}, bf16[4,16,2048]{2,1,0:T(8,128)(2,1)}, f32[16,176]{1,0:T(8,128)}, f32[16,176]{1,0:T(8,128)}) custom-call(bf16[8,2,16,176,256]{4,3,2,1,0:T(8,128)(2,1)S(1)} %get-tuple-element.14.recv, bf16[4,16,2048]{2,1,0:T(8,128)(2,1)S(1)} %get-tuple-element.15.router, ...), custom_call_target="tpu_custom_call" | custom-call | tf_op jit(solution)/shard_map/pallas_call | solution.py:242
Async XLA Ops:
  0.6 0.7 copy-start
  1.4 0.7 copy-start.1
